TPU v7x, 512 devices: a whole 4x4x16 slice. The times are simulated.
512 devices in a mesh: runner: 16 (over z), cells: 32 (over x, y, core).
Axes of the slice: x: 4, y: 4, z: 16, core: 2. Of those that a mesh axis runs over, the one named last changes fastest.
Arguments:
- states: float32 [2048, 256, 128], P('runner', 'cells'), may hold values from -4 to 4
- diffusivity: float32 [256, 128], P('cells'), may hold values from 0.03 to 0.2
- velocity: float32 [2, 256, 128], P(None, 'cells'), may hold values from -0.15 to 0.15
- counts: int32 [16], replicated, may hold values from 1 to 128, 1024 in all
- obs_index: int32 [16384], P('cells'), may hold values from 0 to 1023
- obs_value: float32 [16384], P('cells'), may hold values from -6 to 6
- obs_weight: float32 [16384], P('cells'), may hold values from 0.3 to 3
Outputs:
- analysed: float32 [2048, 256, 128], P('runner', 'cells')
Inputs may be any that keep to these rules, and one draw needn't show every extreme that they name: Runner r's members fill its first counts[r] slots, in runner order; the counts sum to 1024 and the largest is exactly 128. Observation k lies in the rows of cells index k // 512; obs_index counts cells within those 8 x 128 cells, row by row; a cell may be observed more than once.
All inputs are finite; a program needn't handle non-finite values.
Results may differ from a plain program's by a relative error of at most 0.013.
Values may be sent and summed in bfloat16 or wider, within the bound.
A program may use at most 64 MiB of HBM per device.

v0:
```python
import math

import jax
import jax.numpy as jnp
from jax import lax
from jax.sharding import PartitionSpec as P

STEPS = 4


def with_halo(block, sides, width):
    for axis, dim in sides:
        count = lax.axis_size(axis)
        forward = [(i, i + 1) for i in range(count - 1)]
        forward.append((count - 1, 0))
        backward = [(target, source) for source, target in forward]
        low = lax.ppermute(
            lax.slice_in_dim(block, block.shape[dim] - width, None, axis=dim), axis, forward
        )
        high = lax.ppermute(lax.slice_in_dim(block, 0, width, axis=dim), axis, backward)
        block = jnp.concatenate([low, block, high], axis=dim)
    return block


def from_everyone(value, axis):
    size = lax.axis_size(axis)
    return lax.all_to_all(
        jnp.broadcast_to(value[None], (size, *value.shape)), axis, 0, 0, tiled=True
    )


def of_everyone(value, axis):
    everything = from_everyone(value, axis)
    return jnp.sum(everything, axis=0)


def split_up(value, dim, size):
    shape = value.shape
    pieces = value.reshape(*shape[:dim], size, shape[dim] // size, *shape[dim + 1 :])
    return jnp.moveaxis(pieces, dim, 0)


def sent_and_summed(value, axis, dim):
    pieces = split_up(value, dim, lax.axis_size(axis))
    arrived = lax.all_to_all(pieces, axis, split_axis=0, concat_axis=0, tiled=True)
    return arrived.sum(axis=0)


def filled_up(lines, size):
    spare = -len(lines) % size
    return jnp.pad(lines, [(0, spare)] + [(0, 0)] * (lines.ndim - 1))


def in_order(pieces, dim):
    pieces = jnp.moveaxis(pieces, 0, dim)
    shape = pieces.shape
    return pieces.reshape(*shape[:dim], shape[dim] * shape[dim + 1], *shape[dim + 2 :])


def collect(value, axis, dim):
    return in_order(from_everyone(value, axis), dim)


def total_of(value, axes):
    own = sent_and_summed(filled_up(value, lax.axis_size(axes)), axes, 0)
    whole = collect(own, axes, 0)
    return whole[: len(value)].reshape(value.shape)


def in_one(arrays, axis):
    flat, at, gathered = (jnp.concatenate([a.reshape(-1) for a in arrays]), 0, [])
    so_far = total_of(flat, axis)
    for a in arrays:
        gathered.append(so_far[at : at + a.size].reshape(a.shape))
        at += a.size
    return tuple(gathered)


def in_one_piece(arrays, axis, dim, along):
    widths = [math.prod(a.shape[along:]) for a in arrays]
    both = jnp.concatenate(
        [a.reshape(*a.shape[:along], w) for a, w in zip(arrays, widths)], axis=along
    )
    out = lax.all_gather(both, axis, axis=dim, tiled=True)
    pieces = jnp.split(out, [sum(widths[:k]) for k in range(1, len(widths))], axis=along)
    return tuple((b.reshape(*out.shape[:along], *a.shape[along:]) for a, b in zip(arrays, pieces)))


def update(values, upper_row, lower_row, diffusivity, velocity_rows, velocity_cols):
    right_col = jnp.roll(values, -1, axis=2)
    left_col = jnp.roll(values, 1, axis=2)
    laplace = upper_row + lower_row + right_col + left_col - 4.0 * values
    return (
        values
        + diffusivity * laplace
        - 0.5 * velocity_rows * (upper_row - lower_row)
        - 0.5 * velocity_cols * (right_col - left_col)
        - 0.05 * values * values * values
    )


def body(states, diffusivity, velocity, counts, obs_index, obs_value, obs_weight):
    runners = lax.axis_size("runner")
    slot_count = states.shape[0]
    rows_own = states.shape[1]
    members = slot_count // 2 * runners
    values = states
    extended = with_halo(values.astype(jnp.bfloat16), (("cells", 1),), STEPS).astype(values.dtype)
    fields = jnp.concatenate([diffusivity[None], velocity], axis=0)
    wide_fields = with_halo(fields, (("cells", 1),), STEPS)
    for iteration in range(STEPS):
        inner = extended.shape[1] - 2
        first = iteration + 1
        local = wide_fields[:, first : first + inner, :]
        extended = update(
            extended[:, 1:-1, :],
            extended[:, 2:, :],
            extended[:, :-2, :],
            local[0],
            local[1],
            local[2],
        )
    values = extended
    runner_rank = lax.axis_index("runner")
    run_ends = jnp.cumsum(counts)
    offsets = run_ends - counts
    run_ids = jnp.arange(runners, dtype=jnp.int32)
    picker = run_ids == runner_rank
    own_count = jnp.sum(jnp.where(picker, counts, 0))
    own_base = jnp.sum(jnp.where(picker, offsets, 0))
    position = jnp.arange(slot_count, dtype=jnp.int32)
    is_live = position < own_count
    flat_rows = values.reshape(slot_count, -1)
    live_sum = jnp.sum(jnp.where(is_live[:, None], flat_rows, 0.0), axis=0)
    ensemble_mean = of_everyone(live_sum, "runner") / members
    member_deviation = jnp.where(is_live[:, None], flat_rows - ensemble_mean, 0.0).astype(
        jnp.bfloat16
    )
    member_ids = jnp.arange(members, dtype=jnp.int32)
    owner_run = jnp.sum((run_ends[None, :] <= member_ids[:, None]).astype(jnp.int32), axis=1)
    owner_off = jnp.sum(
        jnp.where(owner_run[:, None] == run_ids[None, :], offsets[None, :], 0), axis=1
    )
    slot_of = owner_run * slot_count + member_ids - owner_off
    own_obs = jnp.take(member_deviation, obs_index, axis=1)
    gathered = lax.all_gather(member_deviation, "runner", axis=0, tiled=True)
    compact = jnp.take(gathered, slot_of, axis=0)
    observed = jnp.take(compact, obs_index, axis=1)
    weighted = (own_obs.astype(jnp.float32) * obs_weight).astype(jnp.bfloat16)
    gram_part = lax.dot_general(
        weighted, observed, (((1,), (1,)), ((), ())), preferred_element_type=jnp.float32
    )
    innovation = obs_value - jnp.take(ensemble_mean, obs_index)
    bias_part = jnp.dot(weighted.astype(jnp.float32), innovation, precision=lax.Precision.HIGHEST)
    gram_rows, bias_rows = in_one((gram_part, bias_part), "cells")
    member_col = own_base + position
    column = jnp.clip(member_col, 0, members - 1)
    diagonal = jnp.take_along_axis(gram_rows, column[:, None], axis=1)[:, 0]
    trace_sum = of_everyone(jnp.sum(jnp.where(is_live, diagonal, 0.0)), "runner")
    scaling = members / trace_sum
    scaled_own = (gram_rows * scaling).astype(jnp.bfloat16)
    bias_own = (bias_rows * scaling).astype(jnp.bfloat16)
    scaled_all, bias_all = in_one_piece((scaled_own, bias_own), "runner", 0, 1)
    scaled_full = jnp.take(scaled_all, slot_of, axis=0)
    bias_full = jnp.take(bias_all, slot_of, axis=0)
    square = jnp.dot(scaled_own, scaled_full, preferred_element_type=jnp.float32).astype(
        jnp.bfloat16
    )
    cubed = jnp.dot(square, scaled_full, preferred_element_type=jnp.float32)
    identity = jnp.where(
        is_live[:, None] & (member_ids[None, :] == member_col[:, None]), 1.0, 0.0
    ).astype(jnp.float32)
    transform = (
        1.0 * identity
        - 0.5 * scaled_own.astype(jnp.float32)
        + 0.375 * square.astype(jnp.float32)
        - 0.3125 * cubed
    )
    shift_weights = jnp.dot(
        transform, bias_full.astype(jnp.float32), precision=lax.Precision.HIGHEST
    )
    increment = of_everyone(
        jnp.dot(
            shift_weights, member_deviation.astype(jnp.float32), precision=lax.Precision.HIGHEST
        ),
        "runner",
    )
    narrow = transform.astype(jnp.bfloat16)
    applied = jnp.dot(narrow, compact, preferred_element_type=jnp.float32)
    result = jnp.where(is_live[:, None], ensemble_mean + increment + applied, 0.0)
    return result.reshape(slot_count, rows_own, -1)


def solution(mesh):
    return jax.shard_map(
        body,
        mesh=mesh,
        in_specs=(
            P("runner", "cells", None),
            P("cells", None),
            P(None, "cells", None),
            P(),
            P("cells"),
            P("cells"),
            P("cells"),
        ),
        out_specs=P("runner", "cells", None),
        check_vma=False,
    )
```

profile of v0, /device:TPU:2, one launch (start us, length us, event | category | flops | bytes accessed | tf_op | source)
XLA Modules:
  0.0 331.2 jit_solution(4801979471632581881)
XLA Ops:
  6.5 0.8 fusion.21
  7.3 1.9 collective-permute-start.2
  9.2 5.8 %collective-permute-start.3 = (f32[3,4,128]{2,1,0:T(4,128)S(1)}, f32[3,4,128]{2,1,0:T(4,128)S(1)}, u32[]{:S(2)}, u32[]{:S(2)}) collective-permute-start(f32[3,4,128]{2,1,0:T(4,128)S(1)} %get-tuple-element.40), channel_id=1, source_target_pairs={{1,0},{2,1},{3,2},{4,3},{5,4},{6,5},{7,6},{8,7},{9,8},{10,9},{11,1... | collective-permute-start | bytes 18440 | tf_op jit(solution)/shard_map/ppermute | solution.py:20
  15.0 1.1 convert_element_type.39
  16.2 1.9 collective-permute-start
  18.1 5.8 %collective-permute-start.1 = (bf16[128,4,128]{2,1,0:T(4,128)(2,1)S(1)}, bf16[128,4,128]{2,1,0:T(4,128)(2,1)S(1)}, u32[]{:S(2)}, u32[]{:S(2)}) collective-permute-start(bf16[128,4,128]{2,1,0:T(4,128)(2,1)S(1)} %get-tuple-element.29), channel_id=1, source_target_pairs={{1,0},{2,1},{3,2},{4,3},{5,4},{6,5},{7,6},{8,7},{9,8},{10,9},{11,1... | collective-permute-start | bytes 393224 | tf_op jit(solution)/shard_map/ppermute | solution.py:20
  23.9 0.7 multiply_bitcast_fusion.1
  24.6 0.7 copy.21
  25.5 1.3 fusion.23
  26.8 0.6 iota_compare_fusion.3
  27.4 0.7 pad_maximum_fusion.10
  29.2 1.2 fusion.3
  31.2 1.2 fusion.4
  33.1 1.2 fusion.5
  35.0 0.6 select_reduce_fusion
  35.7 27.8 %all_to_all.33 = f32[16,1,1024]{2,1,0:T(1,128)S(1)} all-to-all(f32[16,1,1024]{2,1,0:T(1,128)S(1)} %broadcast_in_dim.156), channel_id=1, replica_groups=mesh['runner'=16,'cells'=32] {'runner'}, dimensions={0} | all-to-all | bytes 131072 | tf_op jit(solution)/shard_map/all_to_all | solution.py:27
  63.5 0.8 fusion.10
  64.6 1.1 copy.22
  65.8 2.3 gather_fusion.2
  68.1 1.3 gather_fusion
  69.8 63.6 %all-gather.3.cloned.1.call-done = bf16[2048,1024]{1,0:T(8,128)(2,1)} async-done(((bf16[128,1024]{1,0:T(8,128)(2,1)}), bf16[2048,1024]{1,0:T(8,128)(2,1)}) %all-gather.3.cloned.1.call-update) | async-done | bytes 4194320 | tf_op jit(solution)/shard_map/all_gather | solution.py:146
  133.4 7.7 %gather_fusion.5 = bf16[1024,1024]{1,0:T(8,128)(2,1)S(1)} fusion(bf16[2048,1024]{1,0:T(8,128)(2,1)} %all-gather.3.cloned.1.call-done, s32[1024]{0:T(1024)S(1)} %get-tuple-element.44), kind=kCustom, calls=%fused_computation.clone | custom fusion | bytes 4198400 | tf_op jit(solution)/shard_map/jit(_take)/gather | solution.py:147
  141.1 1.6 broadcast_select_fusion.1
  142.8 2.9 copy.23
  145.6 2.1 gather_fusion.1
  147.7 0.7 convolution_bitcast_fusion
  148.5 0.7 all_to_all.23
  149.2 17.1 %all_to_all.34 = f32[32,1,4100]{2,1,0:T(1,128)S(1)} all-to-all(f32[32,1,4100]{2,1,0:T(1,128)S(1)} %all_to_all.23), channel_id=1, replica_groups=mesh['runner'=16,'cells'=32] {'cells'}, dimensions={0} | all-to-all | bytes 1049600 | tf_op jit(solution)/shard_map/all_to_all | solution.py:45
  166.7 1.1 broadcast_in_dim.167
  167.7 5.5 %all-to-all-start.2 = ((f32[32,1,4100]{2,1,0:T(1,128)}), f32[32,1,4100]{2,1,0:T(1,128)S(1)}, u32[]{:S(2)}, u32[]{:S(2)}) async-start(f32[32,1,4100]{2,1,0:T(1,128)} %broadcast_in_dim.167), calls=%async_computation.2 | async-start | bytes 1081344 | tf_op jit(solution)/shard_map/all_to_all | solution.py:27
  173.3 0.6 compare_select_fusion.3
  173.9 9.2 %all-to-all-done.2 = f32[32,1,4100]{2,1,0:T(1,128)S(1)} async-done(((f32[32,1,4100]{2,1,0:T(1,128)}), f32[32,1,4100]{2,1,0:T(1,128)S(1)}, u32[]{:S(2)}, u32[]{:S(2)}) %all-to-all-start.2) | async-done | bytes 524832 | tf_op jit(solution)/shard_map/all_to_all | solution.py:27
  183.1 1.3 reduce.6
  184.8 1.5 gather_fusion.4
  186.3 1.9 fusion.27
  188.2 0.6 broadcast_in_dim.170
  188.8 19.6 %all_to_all.35 = f32[16,1,1]{2,1,0:T(1,128)S(1)} all-to-all(f32[16,1,1]{2,1,0:T(1,128)S(1)} %broadcast_in_dim.170), channel_id=1, replica_groups=mesh['runner'=16,'cells'=32] {'runner'}, dimensions={0} | all-to-all | bytes 128 | tf_op jit(solution)/shard_map/all_to_all | solution.py:27
  208.4 0.6 reduce_sum.100
  209.9 0.7 pad_maximum_fusion.9
  211.3 67.8 %all-gather.5.cloned.1.call-done = bf16[2048,1025]{1,0:T(8,128)(2,1)} async-done(((bf16[128,1025]{1,0:T(8,128)(2,1)}), bf16[2048,1025]{1,0:T(8,128)(2,1)}) %all-gather.5.cloned.1.call-update) | async-done | bytes 4198416 | tf_op jit(solution)/shard_map/all_gather | solution.py:84
  279.1 4.6 %split.8 = bf16[2048,1024]{1,0:T(8,128)(2,1)} slice(bf16[2048,1025]{1,0:T(8,128)(2,1)} %all-gather.5.cloned.1.call-done), slice={[0:2048], [0:1024]} | slice | bytes 8388608 | tf_op jit(solution)/shard_map/split | solution.py:85
  283.7 7.7 %gather_fusion.6 = bf16[1024,1024]{1,0:T(8,128)(2,1)S(1)} fusion(bf16[2048,1024]{1,0:T(8,128)(2,1)} %split.8, s32[1024]{0:T(1024)S(1)} %get-tuple-element.44), kind=kCustom, calls=%fused_computation.1.clone | custom fusion | bytes 4198400 | tf_op jit(solution)/shard_map/jit(_take)/gather | solution.py:164
  291.4 1.7 slice_reduce_fusion
  293.1 6.8 %gather_fusion.3 = bf16[1024]{0:T(1024)(128)(2,1)S(1)} fusion(bf16[2048]{0:T(1024)(128)(2,1)S(1)} %slice_reduce_fusion, s32[1024]{0:T(1024)S(1)} %broadcast_clamp_fusion), kind=kCustom, calls=%fused_computation.5 | custom fusion | bytes 8192 | tf_op jit(solution)/shard_map/jit(_take)/gather | solution.py:165
  300.0 0.6 convolution_convert_fusion
  300.6 2.4 fusion.2
  303.6 19.4 %all_to_all.36 = f32[16,1,1024]{2,1,0:T(1,128)S(1)} all-to-all(f32[16,1,1024]{2,1,0:T(1,128)S(1)} %broadcast_in_dim.172), channel_id=1, replica_groups=mesh['runner'=16,'cells'=32] {'runner'}, dimensions={0} | all-to-all | bytes 131072 | tf_op jit(solution)/shard_map/all_to_all | solution.py:27
  323.5 0.9 copy.34
  (71 shorter events, 6.8 us)
Async XLA Ops:
  6.5 126.9 %all-gather.3.cloned.1.call-start = ((), (), s32[]{:S(2)}) async-start(), calls=%async_computation.5 | async-start | bytes 4456448 | tf_op jit(solution)/shard_map/all_gather | solution.py:146
  7.3 20.1 %collective-permute-start.2 = (f32[3,4,128]{2,1,0:T(4,128)S(1)}, f32[3,4,128]{2,1,0:T(4,128)S(1)}, u32[]{:S(2)}, u32[]{:S(2)}) collective-permute-start(f32[3,4,128]{2,1,0:T(4,128)S(1)} %get-tuple-element.39), channel_id=1, source_target_pairs={{0,1},{1,2},{2,3},{3,4},{4,5},{5,6},{6,7},{7,8},{8,9},{9,10},{10,1... | collective-permute-start | bytes 18440 | tf_op jit(solution)/shard_map/ppermute | solution.py:17
  9.2 18.2 %collective-permute-start.3 = (f32[3,4,128]{2,1,0:T(4,128)S(1)}, f32[3,4,128]{2,1,0:T(4,128)S(1)}, u32[]{:S(2)}, u32[]{:S(2)}) collective-permute-start(f32[3,4,128]{2,1,0:T(4,128)S(1)} %get-tuple-element.40), channel_id=1, source_target_pairs={{1,0},{2,1},{3,2},{4,3},{5,4},{6,5},{7,6},{8,7},{9,8},{10,9},{11,1... | collective-permute-start | bytes 18440 | tf_op jit(solution)/shard_map/ppermute | solution.py:20
  16.2 12.0 %collective-permute-start = (bf16[128,4,128]{2,1,0:T(4,128)(2,1)S(1)}, bf16[128,4,128]{2,1,0:T(4,128)(2,1)S(1)}, u32[]{:S(2)}, u32[]{:S(2)}) collective-permute-start(bf16[128,4,128]{2,1,0:T(4,128)(2,1)S(1)} %get-tuple-element.28), channel_id=1, source_target_pairs={{0,1},{1,2},{2,3},{3,4},{4,5},{5,6},{6,7},{7,8},{8,9},{9,10},{10,1... | collective-permute-start | bytes 393224 | tf_op jit(solution)/shard_map/ppermute | solution.py:17
  18.1 10.1 %collective-permute-start.1 = (bf16[128,4,128]{2,1,0:T(4,128)(2,1)S(1)}, bf16[128,4,128]{2,1,0:T(4,128)(2,1)S(1)}, u32[]{:S(2)}, u32[]{:S(2)}) collective-permute-start(bf16[128,4,128]{2,1,0:T(4,128)(2,1)S(1)} %get-tuple-element.29), channel_id=1, source_target_pairs={{1,0},{2,1},{3,2},{4,3},{5,4},{6,5},{7,6},{8,7},{9,8},{10,9},{11,1... | collective-permute-start | bytes 393224 | tf_op jit(solution)/shard_map/ppermute | solution.py:20
  34.3 0.7 copy-start.3
  35.0 29.4 %copy-start.4 = (s32[512]{0:T(512)S(1)}, s32[512]{0:T(512)}, u32[]{:S(2)}) copy-start(s32[512]{0:T(512)} %param.13) | copy-start | bytes 6148
  64.4 5.0 %copy-start.5 = (f32[512]{0:T(512)S(1)}, f32[512]{0:T(512)}, u32[]{:S(2)}) copy-start(f32[512]{0:T(512)} %param.14) | copy-start | bytes 6148
  64.4 5.1 %copy-start.6 = (f32[512]{0:T(512)S(1)}, f32[512]{0:T(512)}, u32[]{:S(2)}) copy-start(f32[512]{0:T(512)} %param.15) | copy-start | bytes 6148
  167.7 15.4 %all-to-all-start.2 = ((f32[32,1,4100]{2,1,0:T(1,128)}), f32[32,1,4100]{2,1,0:T(1,128)S(1)}, u32[]{:S(2)}, u32[]{:S(2)}) async-start(f32[32,1,4100]{2,1,0:T(1,128)} %broadcast_in_dim.167), calls=%async_computation.2 | async-start | bytes 1081344 | tf_op jit(solution)/shard_map/all_to_all | solution.py:27
  173.2 105.8 %all-gather.5.cloned.1.call-start = ((), (), s32[]{:S(2)}) async-start(), calls=%async_computation.6 | async-start | bytes 5013504 | tf_op jit(solution)/shard_map/all_gather | solution.py:84
  291.4 8.5 %copy-start.2 = (bf16[1024,1024]{1,0:T(8,128)(2,1)}, bf16[1024,1024]{1,0:T(8,128)(2,1)S(1)}, u32[]{:S(2)}) copy-start(bf16[1024,1024]{1,0:T(8,128)(2,1)S(1)} %gather_fusion.6) | copy-start | bytes 6291460
  300.5 2.8 copy-start.1
  300.5 22.5 %copy-start = (bf16[1024,1024]{1,0:T(8,128)(2,1)S(1)}, bf16[1024,1024]{1,0:T(8,128)(2,1)}, u32[]{:S(2)}) copy-start(bf16[1024,1024]{1,0:T(8,128)(2,1)} %broadcast_select_fusion.1) | copy-start | bytes 6291460
Sparse Core Ops, SparseCore 0:
  64.5 68.8 all-gather.2
  210.8 68.1 all-gather.4
where the time goes:
time: 332 us; the launch traced here: 331 us
  waiting for transfers between devices  141 us (42%)
  blocking collectives  84 us (25%)
  local copies, waits for them, and re-layouts  47.3 us (14%)
  starting transfers between devices  20.9 us (6%)
  other arithmetic  18.7 us (6%)
  between operations  14.7 us (4%)
  matrix products  4.98 us (2%)
    all_gather x1, waiting for transfers between devices, in_one_piece(): out = lax.all_gather(both, axis, axis=dim, tiled=True)  67.8 us
    all_to_all x3, blocking collectives, from_everyone(): lax.all_to_all(jnp.broadcast_to(value[None], (size, *value.shape)), axis,...  66.8 us
    all_gather x1, waiting for transfers between devices, body(): gathered = lax.all_gather(member_deviation, 'runner', axis=0, tiled=True)  63.6 us
    all_to_all x1, blocking collectives, sent_and_summed(): lax.all_to_all(pieces, axis, split_axis=0, concat_axis=0, tiled=True)  17.1 us
    ppermute x2, starting transfers between devices, with_halo(): lax.ppermute(lax.slice_in_dim(block, 0, width, axis=dim), axis, backward)  11.5 us
    all_to_all x1, waiting for transfers between devices, from_everyone(): lax.all_to_all(jnp.broadcast_to(value[None], (size, *value.shape)), axis,...  9.25 us
    gather x1, local copies, waits for them, and re-layouts, body(): compact = jnp.take(gathered, slot_of, axis=0)  7.7 us
    gather x1, local copies, waits for them, and re-layouts, body(): scaled_full = jnp.take(scaled_all, slot_of, axis=0)  7.7 us
  transfers between devices with their start and end apart: 7, of which 3 were waited for; matrix products, arithmetic and copies ran while one was open for 4% of the time, Pallas kernels for 0%

commit v1 on v0

v1 whole, which is shorter than its diff:
```python
import functools

import jax
import jax.numpy as jnp
from jax import lax
from jax.experimental import pallas as pl
from jax.experimental.pallas import tpu as pltpu
from jax.sharding import PartitionSpec as P

MESH = pl.DeviceIdType.MESH
STEPS = 4
F32 = jnp.float32
BF16 = jnp.bfloat16
VMEM = pltpu.VMEM
DMA = pltpu.SemaphoreType.DMA


def split3(x):
    hi = x.astype(BF16)
    rest = x - hi.astype(F32)
    mid = rest.astype(BF16)
    low = (rest - mid.astype(F32)).astype(BF16)
    return hi, mid, low


def rows_of(parts, rows):
    have = sum(p.shape[0] for p in parts)
    if have < rows:
        parts = list(parts) + [jnp.zeros((rows - have, parts[0].shape[1]), parts[0].dtype)]
    return jnp.concatenate(parts, axis=0)


def dot(a, b):
    return lax.dot_general(a, b, (((1,), (0,)), ((), ())), preferred_element_type=F32)


def dot_t(a, b):
    return lax.dot_general(a, b, (((1,), (1,)), ((), ())), preferred_element_type=F32)


def halo_kernel(cells, st, fl, prev_out, next_out, fprev_out, fnext_out, hi_s, lo_s, fhi_s, flo_s, ssem, rsem):
    me = lax.axis_index("cells")
    nxt = lax.rem(me + 1, cells)
    prv = lax.rem(me + cells - 1, cells)
    barrier = pltpu.get_barrier_semaphore()
    for who in (nxt, prv):
        pl.semaphore_signal(barrier, inc=1, device_id={"cells": who}, device_id_type=MESH)
    width = st.shape[2]
    rows = st.shape[1]
    for k in range(STEPS):
        cols = slice(k * width, (k + 1) * width)
        lo_s[:, cols] = st[:, k, :].astype(BF16)
        hi_s[:, cols] = st[:, rows - STEPS + k, :].astype(BF16)
    for f in range(3):
        flo_s[f] = fl[f, 0:STEPS, :]
        fhi_s[f] = fl[f, rows - STEPS : rows, :]
    pl.semaphore_wait(barrier, 2)
    copies = []
    for n, (src, dst, who) in enumerate(
        ((hi_s, prev_out, nxt), (lo_s, next_out, prv), (fhi_s, fprev_out, nxt), (flo_s, fnext_out, prv))
    ):
        copies.append(
            pltpu.make_async_remote_copy(
                src_ref=src, dst_ref=dst, send_sem=ssem.at[n], recv_sem=rsem.at[n],
                device_id={"cells": who}, device_id_type=MESH,
            )
        )
    for copy in copies:
        copy.start()
    for copy in copies:
        copy.wait()


def main_kernel(
    R, C,
    st, hprev, hnext, fl, fprev, fnext, counts, obs_idx, obs_val, obs_w,
    out,
    cf, fc, offs, qt, pt, abuf, ap, lmb, gp, rsb, bsb, brow, gs, sz, sb,
    lm_s, lm_r, ring_s, ring_r, rs_s, rs_r, b_s, b_r, z_s, z_r, pl_s, pl_r, rl_s, rl_r,
):
    SL, X, Y = st.shape
    CELLS = X * Y
    M = SL // 2 * R
    PAD = SL * R
    H = CELLS // 2
    NJ = C // 4
    HALF = R // 2
    NCH = C // 2
    OBS = obs_idx.shape[1]
    me = lax.axis_index("runner")
    mec = lax.axis_index("cells")
    core = lax.rem(mec, 2)
    chip = mec // 2

    barrier = pltpu.get_barrier_semaphore()

    def greet_z(d, _):
        pl.semaphore_signal(barrier, inc=1, device_id={"runner": lax.rem(me + d, R)}, device_id_type=MESH)
        return 0

    def greet_c(d, _):
        pl.semaphore_signal(barrier, inc=1, device_id={"cells": lax.rem(mec + d, C)}, device_id_type=MESH)
        return 0

    lax.fori_loop(1, R, greet_z, 0)
    lax.fori_loop(1, C, greet_c, 0)

    total = jnp.int32(0)
    for q in range(R):
        offs[q] = total
        total = total + counts[q]
    own = counts[me]

    for k in range(X + 2 * STEPS):
        if k < STEPS:
            d, v0, v1 = (fprev[f, k : k + 1, :] for f in range(3))
        elif k < STEPS + X:
            d, v0, v1 = (fl[f, k - STEPS : k - STEPS + 1, :] for f in range(3))
        else:
            d, v0, v1 = (fnext[f, k - STEPS - X : k - STEPS - X + 1, :] for f in range(3))
        cf[0, k : k + 1, :] = d - 0.5 * v0
        cf[1, k : k + 1, :] = d + 0.5 * v0
        cf[2, k : k + 1, :] = d - 0.5 * v1
        cf[3, k : k + 1, :] = d + 0.5 * v1
        cf[4, k : k + 1, :] = 1.0 - 4.0 * d

    def march(g, _):
        sl = pl.ds(pl.multiple_of(g * 16, 16), 16)
        u = [hprev[sl, k * Y : (k + 1) * Y].astype(F32) for k in range(STEPS)]
        u += [st[sl, k, :] for k in range(X)]
        u += [hnext[sl, k * Y : (k + 1) * Y].astype(F32) for k in range(STEPS)]
        for step in range(STEPS):
            new = []
            for k in range(1, len(u) - 1):
                row = k + step
                c = u[k]
                right = pltpu.roll(c, Y - 1, 1)
                left = pltpu.roll(c, 1, 1)
                acc = cf[0, row : row + 1, :] * u[k + 1] + cf[1, row : row + 1, :] * u[k - 1]
                acc = acc + cf[2, row : row + 1, :] * right + cf[3, row : row + 1, :] * left
                acc = acc + c * (cf[4, row : row + 1, :] - 0.05 * (c * c))
                new.append(acc)
            u = new
        for k in range(X):
            fc[sl, k * Y : (k + 1) * Y] = u[k]
        return 0

    lax.fori_loop(0, SL // 16, march, 0)

    slot = lax.broadcasted_iota(jnp.int32, (SL, 1), 0)
    live = slot < own
    lsum = jnp.sum(jnp.where(live, fc[...], 0.0), axis=0, keepdims=True)
    lmean = lsum / own.astype(F32)
    local = jnp.where(live, fc[...] - lmean, 0.0).astype(BF16)

    cell_c = lax.broadcasted_iota(jnp.int32, (CELLS, OBS), 0)
    hot = jnp.where(cell_c == obs_idx[...], 1.0, 0.0).astype(BF16)
    w = obs_w[...]
    ones = jnp.ones((1, OBS), BF16)
    x = rows_of([ones, *split3(w), *split3(w * obs_val[...])], 16)
    sums = dot_t(x, hot)
    flag = sums[0:1] > 0.5
    wsum = sums[1:2] + sums[2:3] + sums[3:4]
    vsum = sums[4:5] + sums[5:6] + sums[6:7]
    r_i = lax.broadcasted_iota(jnp.int32, (CELLS, CELLS), 0)
    c_i = lax.broadcasted_iota(jnp.int32, (CELLS, CELLS), 1)
    upper = jnp.where(r_i < c_i, 1.0, 0.0).astype(BF16)
    flags = jnp.where(flag, 1.0, 0.0)
    before = dot(rows_of([flags.astype(BF16)], 16), upper)[0:1]
    n_obs = jnp.sum(flags, axis=1, keepdims=True)
    cell_r = lax.broadcasted_iota(jnp.int32, (1, CELLS), 1).astype(F32)
    place = jnp.where(flag, before, n_obs + cell_r - before).astype(jnp.int32)
    pt[...] = jnp.where(r_i == place, 1.0, 0.0).astype(BF16)

    moved = dot_t(local, pt[...]).astype(BF16)
    rows3 = rows_of([*split3(lmean), *split3(wsum), *split3(vsum)], 16)
    rows3 = dot_t(rows3, pt[...])
    lmb[me] = rows3[0:1] + rows3[1:2] + rows3[2:3]
    wperm = (rows3[3:4] + rows3[4:5] + rows3[5:6])[:, :H]
    vperm = (rows3[6:7] + rows3[7:8] + rows3[8:9])[:, :H]
    abuf[me, 0] = moved[:, :H]
    abuf[me, 1] = moved[:, H:]

    pl.semaphore_wait(barrier, R + C - 2)

    def lm_copy(d):
        return pltpu.make_async_remote_copy(
            src_ref=lmb.at[me], dst_ref=lmb.at[me], send_sem=lm_s.at[d], recv_sem=lm_r.at[d],
            device_id={"runner": lax.rem(me + d, R)}, device_id_type=MESH,
        )

    def start_lm(d, _):
        lm_copy(d).start()
        return 0

    def wait_lm(d, _):
        lm_copy(d).wait()
        return 0

    SUB = SL // 2

    def ring_copy(h, s, way, sub):
        owner = lax.rem(me - s + R, R) if way == 0 else lax.rem(me + s, R)
        to = lax.rem(me + 1, R) if way == 0 else lax.rem(me + R - 1, R)
        part = abuf.at[owner, h, pl.ds(sub * SUB, SUB)]
        return pltpu.make_async_remote_copy(
            src_ref=part, dst_ref=part,
            send_sem=ring_s.at[way, h, s, sub], recv_sem=ring_r.at[way, h, s, sub],
            device_id={"runner": to}, device_id_type=MESH,
        )

    pieces = [(0, 0), (1, 1), (0, 1), (1, 0)]
    last_pieces = [(0, 0), (1, 1)]

    def ring_start(h):
        for way, sub in pieces if HALF > 1 else last_pieces:
            ring_copy(h, 0, way, sub).start()

    def ring_step(h, s, last=False, before_last=False):
        for way, sub in last_pieces if last else pieces:
            ring_copy(h, s, way, sub).wait_recv()
            if not last and (not before_last or (way, sub) in last_pieces):
                ring_copy(h, s + 1, way, sub).start()

    def ring_sent(h):
        def sent(s, _):
            for way, sub in pieces:
                ring_copy(h, s, way, sub).wait_send()
            return 0

        lax.fori_loop(0, HALF - 1, sent, 0)
        for way, sub in last_pieces:
            ring_copy(h, HALF - 1, way, sub).wait_send()

    ring_start(0)
    lax.fori_loop(1, R, start_lm, 0)

    slots = lax.broadcasted_iota(jnp.int32, (SL, M), 0)
    mems = lax.broadcasted_iota(jnp.int32, (SL, M), 1)

    def build(q, _):
        hit = (mems == slots + offs[q]) & (slots < counts[q])
        qt[pl.ds(pl.multiple_of(q * SL, SL), SL), :] = jnp.where(hit, 1.0, 0.0).astype(BF16)
        return 0

    lax.fori_loop(0, R, build, 0)
    p_i = lax.broadcasted_iota(jnp.int32, (64, SL), 0)
    l_i = lax.broadcasted_iota(jnp.int32, (64, SL), 1)
    wanted = (p_i >> 4) * (16 * R) + 16 * me + (p_i & 15)
    pick = []
    for q in range(R):
        hit = (wanted == l_i + offs[q]) & (l_i < counts[q])
        pick.append(jnp.where(hit, 1.0, 0.0).astype(BF16))
    pick = jnp.concatenate(pick, axis=1)

    lax.fori_loop(1, R, wait_lm, 0)
    mean = jnp.zeros((1, CELLS), F32)
    for q in range(R):
        mean = mean + counts[q].astype(F32) * lmb[q]
    mean = mean / M

    def centre(h, q):
        shift = (lmb[q] - mean)[:, h * H : (h + 1) * H]
        value = abuf[q, h].astype(F32) + shift
        ap[h, pl.ds(pl.multiple_of(q * SL, SL), SL), :] = jnp.where(slot < counts[q], value, 0.0).astype(BF16)

    def run_ring(h, first, last):
        def one(s, _):
            ring_step(h, s)
            centre(h, lax.rem(me - 1 - s + 2 * R, R))
            centre(h, lax.rem(me + 1 + s, R))
            return 0

        if last > first:
            lax.fori_loop(first, last, one, 0)

    def end_ring(h):
        if HALF > 1:
            ring_step(h, HALF - 2, before_last=True)
            centre(h, lax.rem(me - 1 - (HALF - 2) + 2 * R, R))
            centre(h, lax.rem(me + 1 + (HALF - 2), R))

    def finish_ring(h):
        ring_step(h, HALF - 1, last=True)
        centre(h, lax.rem(me + HALF, R))

    centre(0, me)
    run_ring(0, 0, HALF - 2)
    end_ring(0)
    ring_start(1)
    finish_ring(0)

    rows_a = dot(pick, ap[0])
    weighted = (rows_a * wperm).astype(BF16)
    grad = vperm - wperm * mean[:, :H]
    left = jnp.concatenate([weighted, rows_of(list(split3(grad)), 16)], axis=0)
    wide = dot_t(left, ap[0])
    wide_hi = wide.astype(BF16)
    wide_lo = (wide - wide_hi.astype(F32)).astype(BF16)
    both = dot(jnp.concatenate([wide_hi, wide_lo], axis=0), qt[...])
    gram = both[0:80] + both[80:160]
    for c in range(C):
        i, j = c // NJ, c % NJ
        gp[c] = gram[16 * i : 16 * i + 16, 128 * j : 128 * j + 128].astype(BF16)
    bsb[mec] = gram[64:65] + gram[65:66] + gram[66:67]

    def rs_copy(d):
        to = lax.rem(mec + d, C)
        return pltpu.make_async_remote_copy(
            src_ref=gp.at[to], dst_ref=rsb.at[mec], send_sem=rs_s.at[d], recv_sem=rs_r.at[d],
            device_id={"cells": to}, device_id_type=MESH,
        )

    def b_copy(d):
        return pltpu.make_async_remote_copy(
            src_ref=bsb.at[mec], dst_ref=bsb.at[mec], send_sem=b_s.at[d], recv_sem=b_r.at[d],
            device_id={"cells": lax.rem(mec + d, C)}, device_id_type=MESH,
        )

    def start_rs(d, _):
        rs_copy(d).start()
        return 0

    def start_b(d, _):
        b_copy(d).start()
        return 0

    def wait_rs(d, _):
        rs_copy(d).wait()
        return 0

    def wait_b(d, _):
        b_copy(d).wait()
        return 0

    lax.fori_loop(1, C, start_rs, 0)
    lax.fori_loop(1, C, start_b, 0)
    rsb[mec] = gp[mec]

    centre(1, me)
    run_ring(1, 0, min(2, HALF - 2))
    lax.fori_loop(1, C, wait_rs, 0)
    gs[...] = jnp.sum(rsb[...].astype(F32), axis=0).astype(BF16)
    sz[me] = gs[...]

    def z_copy(d):
        return pltpu.make_async_remote_copy(
            src_ref=gs, dst_ref=sz.at[me], send_sem=z_s.at[d], recv_sem=z_r.at[d],
            device_id={"runner": lax.rem(me + d, R)}, device_id_type=MESH,
        )

    def start_z(d, _):
        z_copy(d).start()
        return 0

    def wait_z(d, _):
        z_copy(d).wait()
        return 0

    lax.fori_loop(1, R, start_z, 0)
    run_ring(1, min(2, HALF - 2), min(4, HALF - 2))
    lax.fori_loop(1, R, wait_z, 0)

    def pl_copy(d):
        return pltpu.make_async_remote_copy(
            src_ref=sz, dst_ref=sb.at[mec], send_sem=pl_s.at[d], recv_sem=pl_r.at[d],
            device_id={"cells": lax.rem(chip + d, NCH) * 2 + core}, device_id_type=MESH,
        )

    def relay_copy(d):
        where = lax.rem(chip - d + NCH, NCH) * 2 + core
        return pltpu.make_async_remote_copy(
            src_ref=sb.at[where], dst_ref=sb.at[where], send_sem=rl_s.at[d], recv_sem=rl_r.at[d],
            device_id={"cells": chip * 2 + 1 - core}, device_id_type=MESH,
        )

    def start_pl(d, _):
        pl_copy(d).start()
        return 0

    def relay(d, _):
        pl_copy(d).wait_recv()
        relay_copy(d).start()
        return 0

    def sent_pl(d, _):
        pl_copy(d).wait_send()
        return 0

    def wait_relay(d, _):
        relay_copy(d).wait()
        return 0

    lax.fori_loop(1, NCH, start_pl, 0)
    sb[mec] = sz[...]
    relay_copy(0).start()
    lax.fori_loop(1, C, wait_b, 0)
    bias = jnp.sum(bsb[...], axis=0)
    run_ring(1, min(4, HALF - 2), HALF - 2)
    end_ring(1)
    lax.fori_loop(1, NCH, relay, 0)
    lax.fori_loop(0, NCH, wait_relay, 0)

    def times_gram(left):
        acc = None
        for i in range(4):
            right = jnp.concatenate([sb[i * NJ + j].reshape(16 * R, 128) for j in range(NJ)], axis=1)
            term = dot(left[:, 16 * R * i : 16 * R * (i + 1)], right)
            acc = term if acc is None else acc + term
        return acc

    trace = jnp.zeros((1, 1), F32)
    for i in range(4):
        for j in range(NJ):
            top, end = max(16 * R * i, 128 * j), min(16 * R * (i + 1), 128 * (j + 1))
            if top < end:
                block = sb[i * NJ + j].reshape(16 * R, 128)[top - 16 * R * i : end - 16 * R * i].astype(F32)
                rr = lax.broadcasted_iota(jnp.int32, block.shape, 0) + (top - 128 * j)
                cc = lax.broadcasted_iota(jnp.int32, block.shape, 1)
                part = jnp.where(rr == cc, block, 0.0)
                trace = trace + jnp.sum(jnp.sum(part, axis=0, keepdims=True), axis=1, keepdims=True)
    scaling = M / trace

    eye = qt[pl.ds(pl.multiple_of(me * SL, SL), SL), :]
    bvec = (bias * scaling).astype(BF16)
    one = times_gram(jnp.concatenate([eye, rows_of([bvec], 16)], axis=0)) * scaling
    scaled = one[0:SL].astype(BF16)
    v1 = one[SL : SL + 1]
    two = times_gram(jnp.concatenate([scaled, rows_of(list(split3(v1)), 16)], axis=0)) * scaling
    square = two[0:SL].astype(BF16)
    v2 = two[SL : SL + 1] + two[SL + 1 : SL + 2] + two[SL + 2 : SL + 3]
    three = times_gram(jnp.concatenate([square, rows_of(list(split3(v2)), 16)], axis=0)) * scaling
    cubed = three[0:SL]
    v3 = three[SL : SL + 1] + three[SL + 1 : SL + 2] + three[SL + 2 : SL + 3]
    transform = 1.0 * eye.astype(F32) - 0.5 * scaled.astype(F32) + 0.375 * square.astype(F32) - 0.3125 * cubed
    shift = bvec.astype(F32) - 0.5 * v1 + 0.375 * v2 - 0.3125 * v3
    left = jnp.concatenate([transform.astype(BF16), rows_of(list(split3(shift)), 16)], axis=0)
    left = dot_t(left, qt[...]).astype(BF16)

    finish_ring(1)

    parts = []
    for h in range(2):
        res = dot(left, ap[h])
        inc = res[SL : SL + 1] + res[SL + 1 : SL + 2] + res[SL + 2 : SL + 3]
        parts.append(res[0:SL] + (inc + mean[:, h * H : (h + 1) * H]))
    res = jnp.concatenate(parts, axis=1)
    hi = res.astype(BF16)
    lo = (res - hi.astype(F32)).astype(BF16)
    back = dot(jnp.concatenate([hi, lo], axis=0), pt[...])
    res = jnp.where(live, back[0:SL] + back[SL : 2 * SL], 0.0)
    for k in range(X):
        out[:, k, :] = res[:, k * Y : (k + 1) * Y]

    ring_sent(0)
    ring_sent(1)
    lax.fori_loop(1, NCH, sent_pl, 0)


def body(R, C, states, diffusivity, velocity, counts, obs_index, obs_value, obs_weight):
    SL, X, Y = states.shape
    CELLS = X * Y
    M = SL // 2 * R
    PAD = SL * R
    H = CELLS // 2
    fields = jnp.concatenate([diffusivity[None], velocity], axis=0)
    vm = pl.BlockSpec(memory_space=VMEM)
    hprev, hnext, fprev, fnext = pl.pallas_call(
        functools.partial(halo_kernel, C),
        out_shape=(
            jax.ShapeDtypeStruct((SL, STEPS * Y), BF16),
            jax.ShapeDtypeStruct((SL, STEPS * Y), BF16),
            jax.ShapeDtypeStruct((3, STEPS, Y), F32),
            jax.ShapeDtypeStruct((3, STEPS, Y), F32),
        ),
        in_specs=[vm, vm],
        out_specs=(vm, vm, vm, vm),
        scratch_shapes=[
            VMEM((SL, STEPS * Y), BF16), VMEM((SL, STEPS * Y), BF16),
            VMEM((3, STEPS, Y), F32), VMEM((3, STEPS, Y), F32),
            DMA((4,)), DMA((4,)),
        ],
        compiler_params=pltpu.CompilerParams(collective_id=0, has_side_effects=True),
        name="halo",
    )(states, fields)
    return pl.pallas_call(
        functools.partial(main_kernel, R, C),
        out_shape=jax.ShapeDtypeStruct((SL, X, Y), F32),
        in_specs=[vm] * 6 + [pl.BlockSpec(memory_space=pltpu.SMEM)] + [vm] * 3,
        out_specs=vm,
        scratch_shapes=[
            VMEM((5, X + 2 * STEPS, Y), F32),
            VMEM((SL, CELLS), F32),
            pltpu.SMEM((R,), jnp.int32),
            VMEM((PAD, M), BF16),
            VMEM((CELLS, CELLS), BF16),
            VMEM((R, 2, SL, H), BF16),
            VMEM((2, PAD, H), BF16),
            VMEM((R, 1, CELLS), F32),
            VMEM((C, 16, 128), BF16),
            VMEM((C, 16, 128), BF16),
            VMEM((C, 1, M), F32),
            VMEM((1, M), F32),
            VMEM((16, 128), BF16),
            VMEM((R, 16, 128), BF16),
            VMEM((C, R, 16, 128), BF16),
            DMA((R,)), DMA((R,)),
            DMA((2, 2, R // 2, 2)), DMA((2, 2, R // 2, 2)),
            DMA((C,)), DMA((C,)),
            DMA((C,)), DMA((C,)),
            DMA((R,)), DMA((R,)),
            DMA((C // 2,)), DMA((C // 2,)),
            DMA((C // 2,)), DMA((C // 2,)),
        ],
        compiler_params=pltpu.CompilerParams(
            collective_id=1, has_side_effects=True, vmem_limit_bytes=60 * 1024 * 1024
        ),
        name="cycle",
    )(
        states, hprev, hnext, fields, fprev, fnext, counts,
        obs_index.reshape(1, -1), obs_value.reshape(1, -1), obs_weight.reshape(1, -1),
    )


def solution(mesh):
    sizes = dict(mesh.shape)
    return jax.shard_map(
        functools.partial(body, sizes["runner"], sizes["cells"]),
        mesh=mesh,
        in_specs=(
            P("runner", "cells", None),
            P("cells", None),
            P(None, "cells", None),
            P(),
            P("cells"),
            P("cells"),
            P("cells"),
        ),
        out_specs=P("runner", "cells", None),
        check_vma=False,
    )
```

time: 332 us -> 109 us (0.33)
  the two profiles are of different devices: /device:TPU:2 before, /device:TPU:1 now
where the time goes in v1:
time: 109 us
  Pallas kernels  105 us (96%)
  local copies, waits for them, and re-layouts  2.56 us (2%)
  other arithmetic  1.3 us (1%)
    pallas_call x1, Pallas kernels, body(): pl.pallas_call(functools.partial(main_kernel, R, C), out_shape=jax.ShapeD...  93.7 us
    pallas_call x1, Pallas kernels, body(): pl.pallas_call(functools.partial(halo_kernel, C), out_shape=(jax.ShapeDty...  11.4 us
    unnamed x3, local copies, waits for them, and re-layouts  2.56 us

profile of v1, /device:TPU:1, one launch (start us, length us, event | category | flops | bytes accessed | tf_op | source)
XLA Modules:
  0.0 108.9 jit_solution(4963128822361458244)
XLA Ops:
  0.0 0.0 copy-start
  0.0 0.7 copy-done
  0.7 1.3 %pad_maximum_fusion.fl = f32[3,8,128]{2,1,0:T(8,128)} fusion(f32[2,8,128]{2,1,0:T(8,128)} %param.9, f32[1,8,128]{2,1,0:T(8,128)S(1)} %bitcast.4), kind=kLoop, calls=%fused_computation | loop fusion | flops 3072 | bytes 24576 | tf_op jit(solution)/shard_map/concatenate | solution.py:466
  2.0 11.4 %halo.1 = (bf16[128,512]{1,0:T(8,128)(2,1)}, bf16[128,512]{1,0:T(8,128)(2,1)}, f32[3,4,128]{2,1,0:T(4,128)}, f32[3,4,128]{2,1,0:T(4,128)}) custom-call(f32[128,8,128]{2,1,0:T(8,128)} %st.3, f32[3,8,128]{2,1,0:T(8,128)} %pad_maximum_fusion.fl), custom_call_target="tpu_custom_call" | custom-call | tf_op jit(solution)/shard_map/halo/pallas_call | solution.py:468
  13.3 93.7 %cycle.1 = f32[128,8,128]{2,1,0:T(8,128)} custom-call(f32[128,8,128]{2,1,0:T(8,128)} %st.3, bf16[128,512]{1,0:T(8,128)(2,1)} %get-tuple-element.9.hprev, bf16[128,512]{1,0:T(8,128)(2,1)} %get-tuple-element.10.hnext, f32[3,8,128]{2,1,0:T(8,128)} %pad_maximum_fusion.fl, f32[3,4,128]{2,1,0:T(4,128)} %get-tuple-element.11.fprev, ...), custom_call_target="tpu_custom_call" | custom-call | tf_op jit(solution)/shard_map/cycle/pallas_call | solution.py:486
  107.1 1.9 %copy.9 = f32[128,8,128]{2,1,0:T(8,128)} copy(f32[128,8,128]{2,1,0:T(8,128)} %cycle.1) | data formatting | bytes 1048576
Async XLA Ops:
  0.0 0.7 copy-start

commit v2 on v1

v2 whole, which is shorter than its diff:
```python
import functools

import jax
import jax.numpy as jnp
from jax import lax
from jax.experimental import pallas as pl
from jax.experimental.pallas import tpu as pltpu
from jax.sharding import PartitionSpec as P

MESH = pl.DeviceIdType.MESH
STEPS = 4
T1, T2 = 7, 13
F32 = jnp.float32
BF16 = jnp.bfloat16
VMEM = pltpu.VMEM
DMA = pltpu.SemaphoreType.DMA


def split3(x):
    hi = x.astype(BF16)
    rest = x - hi.astype(F32)
    mid = rest.astype(BF16)
    low = (rest - mid.astype(F32)).astype(BF16)
    return hi, mid, low


def rows_of(parts, rows):
    have = sum(p.shape[0] for p in parts)
    if have < rows:
        parts = list(parts) + [jnp.zeros((rows - have, parts[0].shape[1]), parts[0].dtype)]
    return jnp.concatenate(parts, axis=0)


def dot(a, b):
    return lax.dot_general(a, b, (((1,), (0,)), ((), ())), preferred_element_type=F32)


def dot_t(a, b):
    return lax.dot_general(a, b, (((1,), (1,)), ((), ())), preferred_element_type=F32)


def main_kernel(
    R, C, NSUB,
    st_h, dif_h, vel_h, counts, idx_h, val_h, w_h,
    out,
    st, dif, vel, obs_idx, obs_val, obs_w, in_s,
    hi_s, lo_s, hprev, hnext, fhi_s, flo_s, fprev, fnext,
    cf, fc, offs, qt, pt, abuf, lmb, gp, rsb, bsb, gs, sz, sb, sf,
    level, h_s, h_r, lm_s, lm_r, ring_s, ring_r, rs_s, rs_r, b_s, b_r, z_s, z_r, pl_s, pl_r, pl_rd, rl_s, rl_r,
):
    loads = [
        pltpu.make_async_copy(src, dst, in_s.at[n])
        for n, (src, dst) in enumerate(
            ((st_h, st), (dif_h, dif), (vel_h, vel), (idx_h, obs_idx), (val_h, obs_val), (w_h, obs_w))
        )
    ]
    for load in loads:
        load.start()
    SL, X, Y = st.shape
    CELLS = X * Y
    M = SL // 2 * R
    PAD = SL * R
    H = CELLS // 2
    NJ = C // 4
    HALF = R // 2
    NCH = C // 2
    NY = 4 if NCH >= 16 else 2
    NX = NCH // NY
    OBS = obs_idx.shape[1]
    me = lax.axis_index("runner")
    mec = lax.axis_index("cells")
    core = lax.rem(mec, 2)
    chip = mec // 2
    cx = chip // NY
    cy = lax.rem(chip, NY)
    up = lax.rem(me + 1, R)
    down = lax.rem(me + R - 1, R)
    nxt = lax.rem(mec + 1, C)
    prv = lax.rem(mec + C - 1, C)

    def at(x, y):
        return (lax.rem(x + NX, NX) * NY + lax.rem(y + NY, NY)) * 2 + core

    close = [mec + 1 - 2 * core, at(cx + 1, cy), at(cx - 1, cy), at(cx, cy + 1), at(cx, cy - 1)]

    barrier = pltpu.get_barrier_semaphore()
    for who in (up, down):
        pl.semaphore_signal(barrier, inc=1, device_id={"runner": who}, device_id_type=MESH)
    for who in [nxt, prv] + close:
        pl.semaphore_signal(barrier, inc=1, device_id={"cells": who}, device_id_type=MESH)

    def tell(k):
        for who in close:
            pl.semaphore_signal(level.at[k], inc=1, device_id={"cells": who}, device_id_type=MESH)

    def hear(k):
        pl.semaphore_wait(level.at[k], 5)

    for load in loads:
        load.wait()
    for k in range(STEPS):
        cols = slice(k * Y, (k + 1) * Y)
        lo_s[:, cols] = st[:, k, :].astype(BF16)
        hi_s[:, cols] = st[:, X - STEPS + k, :].astype(BF16)
    flo_s[0] = dif[0:STEPS, :]
    fhi_s[0] = dif[X - STEPS : X, :]
    for f in range(2):
        flo_s[f + 1] = vel[f, 0:STEPS, :]
        fhi_s[f + 1] = vel[f, X - STEPS : X, :]
    pl.semaphore_wait(barrier, 9)

    halo = []
    for n, (src, dst, who) in enumerate(
        ((hi_s, hprev, nxt), (lo_s, hnext, prv), (fhi_s, fprev, nxt), (flo_s, fnext, prv))
    ):
        halo.append(
            pltpu.make_async_remote_copy(
                src_ref=src, dst_ref=dst, send_sem=h_s.at[n], recv_sem=h_r.at[n],
                device_id={"cells": who}, device_id_type=MESH,
            )
        )
    for copy in halo:
        copy.start()
    tell(0)

    total = jnp.int32(0)
    for q in range(R):
        offs[q] = total
        total = total + counts[q]
    own = counts[me]

    cell_c = lax.broadcasted_iota(jnp.int32, (CELLS, OBS), 0)
    hot = jnp.where(cell_c == obs_idx[...], 1.0, 0.0).astype(BF16)
    w = obs_w[...]
    ones = jnp.ones((1, OBS), BF16)
    x = rows_of([ones, *split3(w), *split3(w * obs_val[...])], 16)
    sums = dot_t(x, hot)
    flag = sums[0:1] > 0.5
    wsum = sums[1:2] + sums[2:3] + sums[3:4]
    vsum = sums[4:5] + sums[5:6] + sums[6:7]
    r_i = lax.broadcasted_iota(jnp.int32, (CELLS, CELLS), 0)
    c_i = lax.broadcasted_iota(jnp.int32, (CELLS, CELLS), 1)
    upper = jnp.where(r_i < c_i, 1.0, 0.0).astype(BF16)
    flags = jnp.where(flag, 1.0, 0.0)
    before = dot(rows_of([flags.astype(BF16)], 16), upper)[0:1]
    n_obs = jnp.sum(flags, axis=1, keepdims=True)
    cell_r = lax.broadcasted_iota(jnp.int32, (1, CELLS), 1).astype(F32)
    place = jnp.where(flag, before, n_obs + cell_r - before).astype(jnp.int32)
    pt[...] = jnp.where(r_i == place, 1.0, 0.0).astype(BF16)

    hear(0)
    tell(1)
    for copy in halo:
        copy.wait()

    for k in range(X + 2 * STEPS):
        if k < STEPS:
            d, v0, v1 = (fprev[f, k : k + 1, :] for f in range(3))
        elif k < STEPS + X:
            d = dif[k - STEPS : k - STEPS + 1, :]
            v0, v1 = (vel[f, k - STEPS : k - STEPS + 1, :] for f in range(2))
        else:
            d, v0, v1 = (fnext[f, k - STEPS - X : k - STEPS - X + 1, :] for f in range(3))
        cf[0, k : k + 1, :] = d - 0.5 * v0
        cf[1, k : k + 1, :] = d + 0.5 * v0
        cf[2, k : k + 1, :] = d - 0.5 * v1
        cf[3, k : k + 1, :] = d + 0.5 * v1
        cf[4, k : k + 1, :] = 1.0 - 4.0 * d

    def march(g, _):
        sl = pl.ds(pl.multiple_of(g * 16, 16), 16)
        u = [hprev[sl, k * Y : (k + 1) * Y].astype(F32) for k in range(STEPS)]
        u += [st[sl, k, :] for k in range(X)]
        u += [hnext[sl, k * Y : (k + 1) * Y].astype(F32) for k in range(STEPS)]
        for step in range(STEPS):
            new = []
            for k in range(1, len(u) - 1):
                row = k + step
                c = u[k]
                right = pltpu.roll(c, Y - 1, 1)
                left = pltpu.roll(c, 1, 1)
                acc = cf[0, row : row + 1, :] * u[k + 1] + cf[1, row : row + 1, :] * u[k - 1]
                acc = acc + cf[2, row : row + 1, :] * right + cf[3, row : row + 1, :] * left
                acc = acc + c * (cf[4, row : row + 1, :] - 0.05 * (c * c))
                new.append(acc)
            u = new
        for k in range(X):
            fc[sl, k * Y : (k + 1) * Y] = u[k]
        return 0

    lax.fori_loop(0, SL // 16, march, 0)

    slot = lax.broadcasted_iota(jnp.int32, (SL, 1), 0)
    live = slot < own
    lsum = jnp.sum(jnp.where(live, fc[...], 0.0), axis=0, keepdims=True)
    lmean = lsum / own.astype(F32)
    local = jnp.where(live, fc[...] - lmean, 0.0).astype(BF16)
    moved = dot_t(local, pt[...]).astype(BF16)
    abuf[0, me] = moved[:, :H]
    abuf[1, me] = moved[:, H:]
    rows3 = rows_of([*split3(lmean), *split3(wsum), *split3(vsum)], 16)
    rows3 = dot_t(rows3, pt[...])
    lmb[me] = rows3[0:1] + rows3[1:2] + rows3[2:3]
    wperm = (rows3[3:4] + rows3[4:5] + rows3[5:6])[:, :H]
    vperm = (rows3[6:7] + rows3[7:8] + rows3[8:9])[:, :H]

    SUB = SL // NSUB
    LOW, HIGH = range(NSUB // 2), range(NSUB // 2, NSUB)

    def each(first, last, what):
        def go(d, _):
            what(d)
            return 0

        lax.fori_loop(first, last, go, 0)

    def ring_copy(h, s, way, sub):
        owner = lax.rem(me - s + R, R) if way == 0 else lax.rem(me + s, R)
        part = abuf.at[h, owner, pl.ds(pl.multiple_of(sub * SUB, SUB), SUB)]
        return pltpu.make_async_remote_copy(
            src_ref=part, dst_ref=part, send_sem=ring_s.at[h], recv_sem=ring_r.at[way, h, s, sub],
            device_id={"runner": up if way == 0 else down}, device_id_type=MESH,
        )

    def lm_copy(s, way):
        owner = lax.rem(me - s + R, R) if way == 0 else lax.rem(me + s, R)
        return pltpu.make_async_remote_copy(
            src_ref=lmb.at[owner], dst_ref=lmb.at[owner], send_sem=lm_s, recv_sem=lm_r.at[way, s],
            device_id={"runner": up if way == 0 else down}, device_id_type=MESH,
        )

    def ring_start(h):
        for sub in range(NSUB):
            for way in range(2):
                ring_copy(h, 0, way, sub).start()

    def sub_step(h, s, sub):
        for way in range(2):
            ring_copy(h, s, way, sub).wait_recv()
            ring_copy(h, s + 1, way, sub).start()

    STEPS_H = (HALF - 2) * NSUB

    def ring_run(h, first, last):
        def one(t, _):
            sub_step(h, t // NSUB, lax.rem(t, NSUB))
            return 0

        if last > first:
            lax.fori_loop(first, last, one, 0)

    def ring_tail(h):
        for sub in range(NSUB):
            for way in range(2):
                ring_copy(h, HALF - 2, way, sub).wait_recv()
                if sub in (LOW, HIGH)[way]:
                    ring_copy(h, HALF - 1, way, sub).start()

    def ring_end(h):
        for way in range(2):
            for sub in (LOW, HIGH)[way]:
                ring_copy(h, HALF - 1, way, sub).wait_recv()

    def landed(ref, sem):
        pltpu.make_async_copy(ref, ref, sem).wait()

    for way in range(2):
        lm_copy(0, way).start()
    ring_start(0)
    hear(1)
    tell(2)

    slots = lax.broadcasted_iota(jnp.int32, (SL, M), 0)
    mems = lax.broadcasted_iota(jnp.int32, (SL, M), 1)

    def build(q):
        hit = (mems == slots + offs[q]) & (slots < counts[q])
        qt[pl.ds(pl.multiple_of(q * SL, SL), SL), :] = jnp.where(hit, 1.0, 0.0).astype(BF16)

    PER = R // max(HALF - 2, 1)

    def first_ring(s, early):
        for way in range(2):
            lm_copy(s, way).wait_recv()
            lm_copy(s + 1, way).start()
        for sub in range(NSUB):
            sub_step(0, s, sub)
        early(s)
        build(2 * s)
        build(2 * s + 1)

    def early_start(s):
        for way in range(2):
            ring_copy(1, 0, way, s).start()

    each(0, NSUB, lambda s: first_ring(s, early_start))
    each(NSUB, HALF - 2, lambda s: first_ring(s, lambda t: sub_step(1, 0, t - NSUB)))
    t0 = HALF - 2 - NSUB
    hear(2)
    tell(3)
    for way in range(2):
        lm_copy(HALF - 2, way).wait_recv()
    lm_copy(HALF - 1, 0).start()
    ring_tail(0)
    sub_step(1, 0, t0)
    for q in range(2 * (HALF - 2), R):
        build(q)
    p_i = lax.broadcasted_iota(jnp.int32, (64, SL), 0)
    l_i = lax.broadcasted_iota(jnp.int32, (64, SL), 1)
    wanted = (p_i >> 4) * (16 * R) + 16 * me + (p_i & 15)
    pick = []
    for q in range(R):
        hit = (wanted == l_i + offs[q]) & (l_i < counts[q])
        pick.append(jnp.where(hit, 1.0, 0.0).astype(BF16))
    pick = jnp.concatenate(pick, axis=1)
    hear(3)
    lm_copy(HALF - 1, 0).wait_recv()
    mean = jnp.zeros((1, CELLS), F32)
    for q in range(R):
        mean = mean + counts[q].astype(F32) * lmb[q]
    mean = mean / M
    shifts = jnp.concatenate([lmb[q] - mean for q in range(R)], axis=0)
    ring_end(0)

    first_half = abuf[0].reshape(PAD, H)
    shift0 = shifts[:, :H]
    rows_a = dot(pick, first_half)
    want = wanted[:, 0:1]
    for q in range(R):
        mine = (want >= offs[q]) & (want < offs[q] + counts[q])
        rows_a = rows_a + jnp.where(mine, shift0[q : q + 1], 0.0)
    weighted = (rows_a * wperm).astype(BF16)
    grad = vperm - wperm * mean[:, :H]
    left = jnp.concatenate([weighted, rows_of(list(split3(grad)), 16)], axis=0)
    wide = dot_t(left, first_half)
    extra = [dot_t(left, part) for part in split3(shift0)]
    extra = extra[0] + extra[1] + extra[2]
    wide = jnp.concatenate([wide[:, q * SL : (q + 1) * SL] + extra[:, q : q + 1] for q in range(R)], axis=1)
    wide_hi = wide.astype(BF16)
    wide_lo = (wide - wide_hi.astype(F32)).astype(BF16)
    both = dot(jnp.concatenate([wide_hi, wide_lo], axis=0), qt[...])
    gram = both[0:80] + both[80:160]
    for c in range(C):
        i, j = c // NJ, c % NJ
        gp[c] = gram[16 * i : 16 * i + 16, 128 * j : 128 * j + 128].astype(BF16)
    bsb[mec] = gram[64:65] + gram[65:66] + gram[66:67]

    def rs_copy(d):
        to = lax.rem(mec + d, C)
        return pltpu.make_async_remote_copy(
            src_ref=gp.at[to], dst_ref=rsb.at[mec], send_sem=rs_s, recv_sem=rs_r,
            device_id={"cells": to}, device_id_type=MESH,
        )

    def b_copy(d):
        return pltpu.make_async_remote_copy(
            src_ref=bsb.at[mec], dst_ref=bsb.at[mec], send_sem=b_s, recv_sem=b_r,
            device_id={"cells": lax.rem(mec + d, C)}, device_id_type=MESH,
        )

    def z_copy(d):
        return pltpu.make_async_remote_copy(
            src_ref=gs, dst_ref=sz.at[me], send_sem=z_s, recv_sem=z_r,
            device_id={"runner": lax.rem(me + d, R)}, device_id_type=MESH,
        )

    diagonal = cx == cy
    piece = jnp.where(cx > cy, 1 - core, core)

    def pl_copy(d, second):
        which = 1 - piece if second else piece
        sem = pl_rd.at[cx] if second else pl_r.at[d]
        return pltpu.make_async_remote_copy(
            src_ref=sz.at[pl.ds(which * (R // 2), R // 2)], dst_ref=sb.at[mec * 2 + which],
            send_sem=pl_s.at[1 if second else 0], recv_sem=sem,
            device_id={"cells": lax.rem(chip + d, NCH) * 2 + core}, device_id_type=MESH,
        )

    def relay_copy(where):
        return pltpu.make_async_remote_copy(
            src_ref=sb.at[where], dst_ref=sb.at[where], send_sem=rl_s, recv_sem=rl_r,
            device_id={"cells": chip * 2 + 1 - core}, device_id_type=MESH,
        )

    def first_piece(who):
        wx, wy = who // NY, lax.rem(who, NY)
        return (who * 2 + core) * 2 + jnp.where(wx > wy, 1 - core, core)

    def second_piece(n):
        return ((n * NY + n) * 2 + core) * 2 + 1 - core

    each(1, C, lambda d: rs_copy(d).start())
    rsb[mec] = gp[mec]
    each(1, C, lambda d: b_copy(d).start())

    t1, t2 = T1, T2
    ring_run(1, t0 + 1, t1)
    landed(rsb.at[pl.ds(0, C - 1)], rs_r)
    gs[...] = jnp.sum(rsb[...].astype(F32), axis=0).astype(BF16)
    sz[me] = gs[...]
    each(1, R, lambda d: z_copy(d).start())
    ring_run(1, t1, t2)
    landed(sz.at[pl.ds(0, R - 1)], z_r)

    each(1, NCH, lambda d: pl_copy(d, False).start())

    @pl.when(diagonal)
    def _():
        each(1, NCH, lambda d: pl_copy(d, True).start())

    sb[mec * 2] = sz[0 : R // 2]
    sb[mec * 2 + 1] = sz[R // 2 : R]
    relay_copy(first_piece(chip)).start()

    @pl.when(diagonal)
    def _():
        relay_copy(second_piece(cx)).start()

    landed(bsb.at[pl.ds(0, C - 1)], b_r)
    bias = jnp.sum(bsb[...], axis=0)
    ring_run(1, t2, STEPS_H)
    ring_tail(1)

    def relay(d):
        pltpu.make_async_copy(sb.at[0], sb.at[0], pl_r.at[d]).wait()
        relay_copy(first_piece(lax.rem(chip - d + NCH, NCH))).start()

    each(1, NCH, relay)
    for n in range(NX):

        @pl.when(chip != n * NY + n)
        def _():
            landed(sb.at[0], pl_rd.at[n])
            relay_copy(second_piece(n)).start()

    landed(sb.at[pl.ds(0, NCH + NX)], rl_r)

    def part(x, y, k, half):
        return sb[((x * NY + y) * 2 + k) * 2 + half].reshape(128, 128)

    for x in range(NX):
        sf[256 * x : 256 * x + 128, 256 * x : 256 * x + 128] = part(x, x, 0, 0)
        sf[256 * x + 128 : 256 * x + 256, 256 * x : 256 * x + 128] = part(x, x, 0, 1)
        sf[256 * x : 256 * x + 128, 256 * x + 128 : 256 * x + 256] = part(x, x, 1, 0)
        sf[256 * x + 128 : 256 * x + 256, 256 * x + 128 : 256 * x + 256] = part(x, x, 1, 1)
        for y in range(x + 1, NY):
            for k, half, value in (
                (0, 0, part(x, y, 0, 0)),
                (1, 1, part(x, y, 1, 1)),
            ):
                sf[256 * x + 128 * half : 256 * x + 128 * half + 128, 256 * y + 128 * k : 256 * y + 128 * k + 128] = value
                sf[256 * y + 128 * k : 256 * y + 128 * k + 128, 256 * x + 128 * half : 256 * x + 128 * half + 128] = value.T
            for k, half, value in (
                (0, 1, part(y, x, 0, 1)),
                (1, 0, part(y, x, 1, 0)),
            ):
                sf[256 * y + 128 * half : 256 * y + 128 * half + 128, 256 * x + 128 * k : 256 * x + 128 * k + 128] = value
                sf[256 * x + 128 * k : 256 * x + 128 * k + 128, 256 * y + 128 * half : 256 * y + 128 * half + 128] = value.T

    def times_gram(left):
        return dot(left, sf[...])

    rr = lax.broadcasted_iota(jnp.int32, (128, 128), 0)
    cc = lax.broadcasted_iota(jnp.int32, (128, 128), 1)
    trace = jnp.zeros((1, 128), F32)
    for x in range(NX):
        for k in range(2):
            trace = trace + jnp.sum(jnp.where(rr == cc, part(x, x, k, k).astype(F32), 0.0), axis=0, keepdims=True)
    trace = jnp.sum(trace, axis=1, keepdims=True)
    scaling = M / trace

    eye = qt[pl.ds(pl.multiple_of(me * SL, SL), SL), :]
    bvec = (bias * scaling).astype(BF16)
    one = times_gram(jnp.concatenate([eye, rows_of([bvec], 16)], axis=0)) * scaling
    scaled = one[0:SL].astype(BF16)
    v1 = one[SL : SL + 1]
    two = times_gram(jnp.concatenate([scaled, rows_of(list(split3(v1)), 16)], axis=0)) * scaling
    square = two[0:SL].astype(BF16)
    v2 = two[SL : SL + 1] + two[SL + 1 : SL + 2] + two[SL + 2 : SL + 3]
    three = times_gram(jnp.concatenate([square, rows_of(list(split3(v2)), 16)], axis=0)) * scaling
    cubed = three[0:SL]
    v3 = three[SL : SL + 1] + three[SL + 1 : SL + 2] + three[SL + 2 : SL + 3]
    transform = 1.0 * eye.astype(F32) - 0.5 * scaled.astype(F32) + 0.375 * square.astype(F32) - 0.3125 * cubed
    shift = bvec.astype(F32) - 0.5 * v1 + 0.375 * v2 - 0.3125 * v3
    left = jnp.concatenate([transform.astype(BF16), rows_of(list(split3(shift)), 16)], axis=0)
    mem_r = lax.broadcasted_iota(jnp.int32, (1, M), 1)
    owner = [(mem_r >= offs[q]) & (mem_r < offs[q] + counts[q]) for q in range(R)]
    owner = jnp.concatenate([jnp.where(o, 1.0, 0.0) for o in owner], axis=0).astype(BF16)
    per_runner = dot_t(left, owner)
    moves = lax.dot_general(
        per_runner, shifts, (((1,), (0,)), ((), ())),
        precision=lax.Precision.HIGHEST, preferred_element_type=F32,
    )
    left = dot_t(left, qt[...]).astype(BF16)

    ring_end(1)

    parts = []
    for h in range(2):
        res = dot(left, abuf[h].reshape(PAD, H)) + moves[:, h * H : (h + 1) * H]
        inc = res[SL : SL + 1] + res[SL + 1 : SL + 2] + res[SL + 2 : SL + 3]
        parts.append(res[0:SL] + (inc + mean[:, h * H : (h + 1) * H]))
    res = jnp.concatenate(parts, axis=1)
    hi = res.astype(BF16)
    lo = (res - hi.astype(F32)).astype(BF16)
    back = dot(jnp.concatenate([hi, lo], axis=0), pt[...])
    res = jnp.where(live, back[0:SL] + back[SL : 2 * SL], 0.0)
    for k in range(X):
        out[:, k, :] = res[:, k * Y : (k + 1) * Y]

    for h in range(2):
        landed(abuf.at[h, pl.ds(0, R - 1)], ring_s.at[h])
    landed(lmb.at[pl.ds(0, R - 1)], lm_s)
    landed(gp.at[pl.ds(0, C - 1)], rs_s)
    landed(bsb.at[pl.ds(0, C - 1)], b_s)
    landed(sz.at[pl.ds(0, R - 1)], z_s)
    landed(sb.at[pl.ds(0, NCH - 1)], pl_s.at[0])

    @pl.when(diagonal)
    def _():
        landed(sb.at[pl.ds(0, NCH - 1)], pl_s.at[1])

    landed(sb.at[pl.ds(0, NCH + NX)], rl_s)


def body(R, C, states, diffusivity, velocity, counts, obs_index, obs_value, obs_weight):
    SL, X, Y = states.shape
    CELLS = X * Y
    M = SL // 2 * R
    PAD = SL * R
    H = CELLS // 2
    NSUB = 4
    vm = pl.BlockSpec(memory_space=VMEM)
    hbm = pl.BlockSpec(memory_space=pltpu.HBM)
    n_obs = obs_index.shape[0]
    return pl.pallas_call(
        functools.partial(main_kernel, R, C, NSUB),
        out_shape=jax.ShapeDtypeStruct((SL, X, Y), F32),
        in_specs=[hbm] * 3 + [pl.BlockSpec(memory_space=pltpu.SMEM)] + [hbm] * 3,
        out_specs=vm,
        scratch_shapes=[
            VMEM((SL, X, Y), F32), VMEM((X, Y), F32), VMEM((2, X, Y), F32),
            VMEM((1, n_obs), jnp.int32), VMEM((1, n_obs), F32), VMEM((1, n_obs), F32),
            DMA((6,)),
            VMEM((SL, STEPS * Y), BF16), VMEM((SL, STEPS * Y), BF16),
            VMEM((SL, STEPS * Y), BF16), VMEM((SL, STEPS * Y), BF16),
            VMEM((3, STEPS, Y), F32), VMEM((3, STEPS, Y), F32),
            VMEM((3, STEPS, Y), F32), VMEM((3, STEPS, Y), F32),
            VMEM((5, X + 2 * STEPS, Y), F32),
            VMEM((SL, CELLS), F32),
            pltpu.SMEM((R,), jnp.int32),
            VMEM((PAD, M), BF16),
            VMEM((CELLS, CELLS), BF16),
            VMEM((2, R, SL, H), BF16),
            VMEM((R, 1, CELLS), F32),
            VMEM((C, 16, 128), BF16),
            VMEM((C, 16, 128), BF16),
            VMEM((C, 1, M), F32),
            VMEM((16, 128), BF16),
            VMEM((R, 16, 128), BF16),
            VMEM((2 * C, R // 2, 16, 128), BF16),
            VMEM((M, M), BF16),
            pltpu.SemaphoreType.REGULAR((4,)),
            DMA((4,)), DMA((4,)),
            DMA, DMA((2, R // 2)),
            DMA((2,)), DMA((2, 2, R // 2, NSUB)),
            DMA, DMA, DMA, DMA, DMA, DMA,
            DMA((2,)), DMA((C // 2,)), DMA((4,)),
            DMA, DMA,
        ],
        compiler_params=pltpu.CompilerParams(
            collective_id=1, has_side_effects=True, vmem_limit_bytes=60 * 1024 * 1024
        ),
        name="cycle",
    )(
        states, diffusivity, velocity, counts,
        obs_index.reshape(1, -1), obs_value.reshape(1, -1), obs_weight.reshape(1, -1),
    )


def solution(mesh):
    sizes = dict(mesh.shape)
    return jax.shard_map(
        functools.partial(body, sizes["runner"], sizes["cells"]),
        mesh=mesh,
        in_specs=(
            P("runner", "cells", None),
            P("cells", None),
            P(None, "cells", None),
            P(),
            P("cells"),
            P("cells"),
            P("cells"),
        ),
        out_specs=P("runner", "cells", None),
        check_vma=False,
    )
```

time: 109 us -> 93.5 us (0.86)
  Pallas kernels: 105 us -> 91.5 us
  other arithmetic: 1.3 us -> 0 us
    pallas_call x2 -> x1, Pallas kernels: 105 us -> 91.5 us  [body(): pl.pallas_call(functools.partial(main_kernel, R, C, NSUB), out_shape=jax....]
    concatenate x1 -> x0, other arithmetic: 1.3 us -> none  [body(): fields = jnp.concatenate([diffusivity[None], velocity], axis=0)]
    unnamed x3 -> x1, local copies, waits for them, and re-layouts: 2.56 us -> 1.87 us
where the time goes in v2:
time: 93.5 us; the launch traced here: 93.3 us
  Pallas kernels  91.5 us (98%)
  local copies, waits for them, and re-layouts  1.87 us (2%)
    pallas_call x1, Pallas kernels, body(): pl.pallas_call(functools.partial(main_kernel, R, C, NSUB), out_shape=jax....  91.5 us

profile of v2, /device:TPU:1, one launch (start us, length us, event | category | flops | bytes accessed | tf_op | source)
XLA Modules:
  0.0 93.3 jit_solution(8470824724666540340)
XLA Ops:
  0.0 91.5 %cycle.1 = f32[128,8,128]{2,1,0:T(8,128)} custom-call(f32[128,8,128]{2,1,0:T(8,128)} %st_h.1, f32[8,128]{1,0:T(8,128)} %dif_h.1, f32[2,8,128]{2,1,0:T(8,128)} %vel_h.1, s32[16]{0:T(128)} %counts.1, s32[1,512]{1,0:T(1,128)} %bitcast.3, f32[1,512]{1,0:T(1,128)} %bitcast.4, f32[1,512]{1,0:T(1,128)} %bitcast.5), custom_call_target="tpu_custom_call" | custom-call | tf_op jit(solution)/shard_map/cycle/pallas_call | solution.py:536
  91.5 1.9 %copy.9 = f32[128,8,128]{2,1,0:T(8,128)} copy(f32[128,8,128]{2,1,0:T(8,128)} %cycle.1) | data formatting | bytes 1048576
